TPU v7x, 64 devices: a 2x2x8 block of a 4x4x8 slice. The times are simulated.
64 devices in a mesh: rep: 8 (over x, y, core), dp: 8 (over z).
Axes of the slice: x: 2, y: 2, z: 8, core: 2. Of those that a mesh axis runs over, the one named last changes fastest.
The devices are a block of a 4x4x8 slice.
Arguments:
- x: bfloat16 [64, 4096, 512], P(('rep', 'dp')), parts along dimension 0
- dy: bfloat16 [64, 4096, 512], P(('rep', 'dp')), parts along dimension 0
- w_gate: bfloat16 [2, 512, 1664], replicated
- w_up: bfloat16 [2, 512, 1664], replicated
- w_down: bfloat16 [2, 1664, 512], replicated
- m_w_gate: float32 [2, 512, 1664], P(None, 'dp')
- m_w_up: float32 [2, 512, 1664], P(None, 'dp')
- m_w_down: float32 [2, 1664, 512], P(None, 'dp')
- v_w_gate: float32 [2, 512, 1664], P(None, 'dp')
- v_w_up: float32 [2, 512, 1664], P(None, 'dp')
- v_w_down: float32 [2, 1664, 512], P(None, 'dp')
Outputs:
- output 1: bfloat16 [16, 512, 1664], P('rep'), parts along dimension 0
- output 2: bfloat16 [16, 512, 1664], P('rep'), parts along dimension 0
- output 3: bfloat16 [16, 1664, 512], P('rep'), parts along dimension 0
- output 4: float32 [16, 512, 1664], P('rep', 'dp'), parts along dimension 0
- output 5: float32 [16, 512, 1664], P('rep', 'dp'), parts along dimension 0
- output 6: float32 [16, 1664, 512], P('rep', 'dp'), parts along dimension 0
- output 7: float32 [16, 512, 1664], P('rep', 'dp'), parts along dimension 0
- output 8: float32 [16, 512, 1664], P('rep', 'dp'), parts along dimension 0
- output 9: float32 [16, 1664, 512], P('rep', 'dp'), parts along dimension 0
There are 8 independent parts. A program takes and returns all parts, laid end to end along the dimension named above; an argument that names none is the same for every part.
All inputs are finite; a program needn't handle non-finite values.
Results may differ from a plain program's by a relative error of at most 0.022.
Values are sent between devices in bfloat16 or wider.
A program may use at most 768 MiB of HBM per device.

v0:
```python
import jax
import jax.numpy as jnp
from jax import lax

NAMES = ("w_gate", "w_up", "w_down")


def matmul(a, w):
    return jnp.dot(a, w, preferred_element_type=jnp.float32).astype(jnp.bfloat16)


def normed(h):
    wide = h.astype(jnp.float32)
    scale = lax.rsqrt(jnp.mean(wide**2, -1, keepdims=True) + 1e-6)
    return (wide * scale).astype(jnp.bfloat16)


def layer(h, w):
    a = normed(h)
    gate = jnp.dot(a, w["w_gate"], preferred_element_type=jnp.float32)
    up = jnp.dot(a, w["w_up"], preferred_element_type=jnp.float32)
    return h + matmul((jax.nn.silu(gate) * up).astype(jnp.bfloat16), w["w_down"])


def adamw(w, m, v, g):
    m = 0.9 * m + 0.1 * g
    v = 0.95 * v + 0.05 * g * g
    step = m * lax.rsqrt(v + 1e-8) + 0.1 * w
    return (w - 0.02 * step).astype(jnp.bfloat16), m, v


def clipped(gradients, sum_of_squares, count):
    factor = jnp.minimum(1.0, 0.5 * lax.rsqrt(sum_of_squares / count + 1e-30))
    return [g * factor for g in gradients]


def stack(weights, h):
    for number in range(weights["w_gate"].shape[0]):
        h = layer(h, {name: w[number] for name, w in weights.items()})
    return h


def solution(mesh):
    groups = mesh.shape["rep"]

    def step(x, dy, *arrays):
        weights, m, v = (arrays[i : i + 3] for i in (0, 3, 6))
        x, dy = (t.reshape(groups, -1, *t.shape[1:]) for t in (x, dy))

        def of_a_group(x, dy):
            _, back = jax.vjp(lambda w: stack(w, x), dict(zip(NAMES, weights, strict=True)))
            by_weights = back(dy)[0]
            gradients = [by_weights[name].astype(jnp.float32) for name in NAMES]
            gradients = clipped(gradients, sum(jnp.sum(g * g) for g in gradients), sum(g.size for g in gradients))
            new = [adamw(w.astype(jnp.float32), m, v, g) for w, m, v, g in zip(weights, m, v, gradients, strict=True)]
            return tuple(one[which] for which in range(3) for one in new)

        return tuple(t.reshape(-1, *t.shape[2:]) for t in jax.vmap(of_a_group)(x, dy))

    return step
```

profile of v0, /device:TPU:22, one launch (start us, length us, event | category | flops | bytes accessed | tf_op | source)
XLA Modules:
  0.0 818.3 jit_solution(8332694533655505702)
XLA Ops:
  10.4 6.6 copy
  17.0 6.4 copy.1
  23.4 12.5 %convolution_convert_fusion.1 = bf16[4096,1664]{1,0:T(8,128)(2,1)} fusion(bf16[1,4096,512]{2,1,0:T(8,128)(2,1)} %param.17, bf16[2,1664,512]{2,1,0:T(8,128)(2,1)S(1)} %copy-done.22), kind=kOutput, calls=%fused_computation.199 | convolution fusion | flops 6986137600 | bytes 19529728 | tf_op jit(solution)/vmap(transpose(jvp()))/dot_general | solution.py:9
  36.0 13.1 %fusion.215 = f32[4096,1664]{1,0:T(8,128)} fusion(bf16[2,512,1664]{2,1,0:T(8,128)(2,1)S(1)} %copy-done.24, bf16[1,4096,512]{2,1,0:T(8,128)(2,1)S(1)} %copy-done.7, f32[4096]{0:T(1024)S(1)} %add_rsqrt_fusion), kind=kOutput, calls=%fused_computation.241 | convolution fusion | flops 6985613312 | bytes 33177600 | tf_op jit(solution)/vmap(jvp())/dot_general | solution.py:20
  49.1 27.4 %fusion.164 = (bf16[1,1,4096,1664]{3,2,1,0:T(8,128)(2,1)}, f32[4096,1664]{1,0:T(8,128)}) fusion(f32[4096,1664]{1,0:T(8,128)} %fusion.215, bf16[2,512,1664]{2,1,0:T(8,128)(2,1)} %param.15, bf16[1,4096,512]{2,1,0:T(8,128)(2,1)} %param.14, f32[4096]{0:T(1024)S(1)} %add_rsqrt_fusion), kind=kOutput, calls=%fused_computation.191 | convolution fusion | flops 7026507776 | bytes 74072064 | tf_op jit(solution)/vmap(jvp())/dot_general | solution.py:21
  76.5 19.6 %copy.4 = bf16[1,1,4096,1664]{2,3,1,0:T(8,128)(2,1)} copy(bf16[1,1,4096,1664]{3,2,1,0:T(8,128)(2,1)} %get-tuple-element.263) | data formatting | bytes 27262976
  96.1 12.3 %fusion.174 = (f32[4096]{0:T(1024)S(1)}, bf16[1,1,4096,512]{2,3,1,0:T(8,128)(2,1)S(1)}) fusion(bf16[2,1664,512]{2,1,0:T(8,128)(2,1)S(1)} %copy-done.22, bf16[1,1,4096,1664]{3,2,1,0:T(8,128)(2,1)} %get-tuple-element.263, bf16[1,4096,512]{1,2,0:T(8,128)(2,1)} %copy), kind=kOutput, calls=%fused_computation.213 | convolution fusion | flops 6989803520 | bytes 23740416 | tf_op jit(solution)/vmap(jvp())/dot_general | solution.py:9
  113.4 13.1 %fusion.203 = f32[4096,1664]{1,0:T(8,128)} fusion(bf16[1,1,4096,512]{2,3,1,0:T(8,128)(2,1)S(1)} %fusion.175, bf16[2,512,1664]{2,1,0:T(8,128)(2,1)S(1)} %copy-done.23), kind=kOutput, calls=%fused_computation.229 | convolution fusion | flops 6979321856 | bytes 33161216 | tf_op jit(solution)/vmap(jvp())/dot_general | solution.py:21
  126.5 38.6 %fusion.153 = (bf16[1,1,4096,1664]{3,2,1,0:T(8,128)(2,1)}, bf16[1,1,4096,1664]{3,2,1,0:T(8,128)(2,1)}, f32[4096,1664]{1,0:T(8,128)}) fusion(f32[4096,1664]{1,0:T(8,128)} %fusion.203, bf16[4096,1664]{1,0:T(8,128)(2,1)} %convolution_convert_fusion.1, bf16[2,512,1664]{2,1,0:T(8,128)(2,1)} %param.12, bf16[1,1,4096,512]{2,3,1,0:T(8,128)(2,1)} %copy-done), kind=kOutput, calls=%fused_computation.175 | convolution fusion | flops 7081558016 | bytes 101318656 | tf_op jit(solution)/vmap(jvp())/dot_general | solution.py:20
  165.1 14.6 %fusion.180 = bf16[4096,512]{0,1:T(8,128)(2,1)} fusion(bf16[1,1,4096,1664]{3,2,1,0:T(8,128)(2,1)} %get-tuple-element.622, bf16[2,512,1664]{2,1,0:T(8,128)(2,1)} %param.15), kind=kOutput, calls=%fused_computation.218 | convolution fusion | flops 6979321856 | bytes 19529728 | tf_op jit(solution)/vmap(transpose(jvp()))/dot_general | solution.py:21
  179.7 12.8 %fusion.176 = (f32[4096]{0:T(1024)S(1)}, bf16[1,1,4096,512]{2,3,1,0:T(8,128)(2,1)}) fusion(bf16[1,1,4096,512]{2,3,1,0:T(8,128)(2,1)} %copy-done.8, bf16[4096,512]{0,1:T(8,128)(2,1)} %fusion.180, bf16[2,512,1664]{2,1,0:T(8,128)(2,1)} %param.12, bf16[1,1,4096,1664]{3,2,1,0:T(8,128)(2,1)S(1)} %copy-done.3), kind=kOutput, calls=%fused_computation.215 | convolution fusion | flops 6989803520 | bytes 27934720 | tf_op jit(solution)/vmap(transpose(jvp()))/dot_general | solution.py:20
  192.5 6.8 fusion.198
  199.2 6.5 copy.5
  205.8 55.2 %while.17 = (bf16[1,1,4096,1664]{2,3,1,0:T(8,128)(2,1)}, bf16[1,1,4096,512]{3,2,1,0:T(8,128)(2,1)}, f32[1,208,512]{2,1,0:T(8,128)S(1)}, f32[1,208,512]{2,1,0:T(8...) while((bf16[1,1,4096,1664]{2,3,1,0:T(8,128)(2,1)}, ...), condition=%wide.windowed_dot_general_cond_rs.5.clone, body=%wide.windowed_dot_general_body_rs.5.clone.sunk | while | flops 3503931392 | bytes 122290848 | solution.py:9
  215.9 5.3 fusion.359
  228.5 7.1 collective-permute-done.22
  243.6 5.3 fusion.359
  254.5 5.5 collective-permute-done.22
  261.6 23.6 %fusion.163 = bf16[1,1,4096,1664]{3,2,1,0:T(8,128)(2,1)} fusion(f32[4096,1664]{1,0:T(8,128)} %fusion.203, f32[4096,1664]{1,0:T(8,128)} %get-tuple-element.267), kind=kLoop, calls=%fused_computation.189 | loop fusion | flops 40894464 | bytes 68157440 | tf_op jit(solution)/vmap(jvp())/convert_element_type | solution.py:22
  285.2 19.7 %copy.2 = bf16[1,1,4096,1664]{2,3,1,0:T(8,128)(2,1)} copy(bf16[1,1,4096,1664]{3,2,1,0:T(8,128)(2,1)} %fusion.163) | data formatting | bytes 27262976
  304.9 6.5 copy.3
  311.4 46.6 %while.16 = (bf16[1,1,4096,1664]{2,3,1,0:T(8,128)(2,1)}, bf16[1,1,4096,512]{3,2,1,0:T(8,128)(2,1)}, f32[1,208,512]{2,1,0:T(8,128)S(1)}, f32[1,208,512]{2,1,0:T(8...) while((bf16[1,1,4096,1664]{2,3,1,0:T(8,128)(2,1)}, ...), condition=%wide.windowed_dot_general_cond_rs.4.clone, body=%wide.windowed_dot_general_body_rs.4.clone.sunk | while | flops 3503931392 | bytes 122290848 | solution.py:9
  351.1 6.0 collective-permute-done.18
  364.3 32.8 %convert_multiply_fusion = (bf16[1,1,4096,1664]{3,2,1,0:T(8,128)(2,1)}, bf16[1,1,4096,1664]{3,2,1,0:T(8,128)(2,1)}) fusion(f32[4096,1664]{1,0:T(8,128)} %fusion.215, f32[4096,1664]{1,0:T(8,128)} %get-tuple-element.264, bf16[2,1664,512]{2,1,0:T(8,128)(2,1)} %param.16, bf16[1,1,4096,512]{2,3,1,0:T(8,128)(2,1)} %fusion.198), kind=kOutput, calls=%fused_computation.170 | convolution fusion | flops 7088373760 | bytes 87687168 | tf_op jit(solution)/vmap(transpose(jvp()))/dot_general | solution.py:9
  397.1 55.2 %while.15 = (bf16[1,1,4096,512]{2,3,1,0:T(8,128)(2,1)}, bf16[1,1,4096,1664]{3,2,1,0:T(8,128)(2,1)}, f32[1,64,1664]{2,1,0:T(8,128)S(1)}, f32[1,64,1664]{2,1,0:T(8...) while((bf16[1,1,4096,512]{2,3,1,0:T(8,128)(2,1)}, ...), condition=%wide.windowed_dot_general_cond_rs.3.clone, body=%wide.windowed_dot_general_body_rs.3.clone.sunk | while | flops 3494494208 | bytes 50987620 | solution.py:21
  402.5 7.3 fusion.343
  414.2 7.3 fusion.345
  430.1 7.3 fusion.343
  441.6 7.3 fusion.345
  453.0 59.2 %while.14 = (bf16[1,1,4096,512]{2,3,1,0:T(8,128)(2,1)}, bf16[1,1,4096,1664]{3,2,1,0:T(8,128)(2,1)}, f32[1,64,1664]{2,1,0:T(8,128)S(1)}, f32[1,64,1664]{2,1,0:T(8...) while((bf16[1,1,4096,512]{2,3,1,0:T(8,128)(2,1)}, ...), condition=%wide.windowed_dot_general_cond_rs.2.clone, body=%wide.windowed_dot_general_body_rs.2.clone.sunk | while | flops 3494494208 | bytes 50987620 | solution.py:21
  459.1 7.3 fusion.335
  474.4 7.3 fusion.337
  492.7 7.3 fusion.335
  504.1 7.3 fusion.337
  512.3 52.9 %while.13 = (bf16[1,1,4096,512]{2,3,1,0:T(8,128)(2,1)}, bf16[1,1,4096,1664]{3,2,1,0:T(8,128)(2,1)}, f32[1,64,1664]{2,1,0:T(8,128)S(1)}, f32[1,64,1664]{2,1,0:T(8...) while((bf16[1,1,4096,512]{2,3,1,0:T(8,128)(2,1)}, ...), condition=%wide.windowed_dot_general_cond_rs.1.clone, body=%wide.windowed_dot_general_body_rs.1.clone.sunk | while | flops 3494494208 | bytes 50987620 | solution.py:20
  517.6 7.3 fusion.327
  529.1 7.3 fusion.329
  544.6 7.3 fusion.327
  556.0 7.3 fusion.329
  565.2 65.0 %while.12 = (bf16[1,1,4096,512]{2,3,1,0:T(8,128)(2,1)}, bf16[1,1,4096,1664]{3,2,1,0:T(8,128)(2,1)}, f32[1,64,1664]{2,1,0:T(8,128)S(1)}, f32[1,64,1664]{2,1,0:T(8...) while((bf16[1,1,4096,512]{2,3,1,0:T(8,128)(2,1)}, ...), condition=%wide.windowed_dot_general_cond_rs.clone, body=%wide.windowed_dot_general_body_rs.clone.sunk | while | flops 3494494208 | bytes 52691584 | solution.py:20
  572.3 7.3 fusion.319
  585.6 7.3 fusion.321
  603.5 7.3 fusion.319
  616.8 7.3 fusion.321
  651.6 15.3 %all-reduce.10 = f32[1]{0:T(128)} all-reduce(f32[1]{0:T(128)} %bitcast.39), channel_id=13, replica_groups=mesh['rep'=8,'dp'=8] {'dp'}, use_global_device_ids=true, to_apply=%region_3.4.clone | all-reduce | flops 1 | bytes 8 | tf_op jit(solution)/vmap()/reduce_sum | solution.py:54
  677.8 36.4 %all-gather.14.cloned.1.call-done = bf16[1,2,1664,512]{3,2,1,0:T(8,128)(2,1)} async-done(((bf16[1,2,208,512]{3,2,1,0:T(8,128)(2,1)}), bf16[1,2,1664,512]{3,2,1,0:T(8,128)(2,1)}) %all-gather.14.cloned.1.call-update) | async-done | bytes 3407888 | tf_op jit(solution)/reshape | solution.py:58
  714.1 44.8 %all-gather.12.cloned.1.call-done = bf16[1,2,512,1664]{3,2,1,0:T(8,128)(2,1)} async-done(((bf16[1,2,64,1664]{3,2,1,0:T(8,128)(2,1)}), bf16[1,2,512,1664]{3,2,1,0:T(8,128)(2,1)}) %all-gather.12.cloned.1.call-update) | async-done | bytes 3407888 | tf_op jit(solution)/reshape | solution.py:58
  758.9 44.8 %all-gather.10.cloned.1.call-done = bf16[1,2,512,1664]{3,2,1,0:T(8,128)(2,1)} async-done(((bf16[1,2,64,1664]{3,2,1,0:T(8,128)(2,1)}), bf16[1,2,512,1664]{3,2,1,0:T(8,128)(2,1)}) %all-gather.10.cloned.1.call-update) | async-done | bytes 3407888 | tf_op jit(solution)/reshape | solution.py:58
  (274 shorter events, 216.0 us)
Async XLA Ops:
  7.2 706.9 %all-gather.14.cloned.1.call-start = ((), (), s32[]{:S(2)}) async-start(), calls=%async_computation.2 | async-start | bytes 3833856 | tf_op jit(solution)/reshape | solution.py:58
  205.8 17.3 %collective-permute-start.20 = (f32[1,208,512]{2,1,0:T(8,128)S(1)}, f32[1,208,512]{2,1,0:T(8,128)S(1)}, u32[]{:S(2)}, u32[]{:S(2)}) collective-permute-start(f32[1,208,512]{2,1,0:T(8,128)S(1)} %broadcast_select_fusion.34), channel_id=35, source_target_pairs={{0,1},{1,2},{2,3},{3,4},{4,5},{5,6},{6,7},{7,0},{8,9},{9,10},{10,1... | collective-permute-start | bytes 1277960 | tf_op jit(solution)/vmap(transpose(jvp()))/dot_general | solution.py:9
  208.1 15.0 %collective-permute-start.21 = (f32[1,208,512]{2,1,0:T(8,128)S(1)}, f32[1,208,512]{2,1,0:T(8,128)S(1)}, u32[]{:S(2)}, u32[]{:S(2)}) collective-permute-start(f32[1,208,512]{2,1,0:T(8,128)S(1)} %broadcast_select_fusion.35), channel_id=34, source_target_pairs={{0,7},{1,0},{2,1},{3,2},{4,3},{5,4},{6,5},{7,6},{8,15},{9,8},{10,9... | collective-permute-start | bytes 1277960 | tf_op jit(solution)/vmap(transpose(jvp()))/dot_general | solution.py:9
  223.2 12.4 %collective-permute-start.22 = (f32[1,208,512]{2,1,0:T(8,128)S(1)}, f32[1,208,512]{2,1,0:T(8,128)S(1)}, u32[]{:S(2)}, u32[]{:S(2)}) collective-permute-start(f32[1,208,512]{2,1,0:T(8,128)S(1)} %get-tuple-element.500), channel_id=37, source_target_pairs={{0,1},{1,2},{2,3},{3,4},{4,5},{5,6},{6,7},{7,0},{8,9},{9,10},{10,1... | collective-permute-start | bytes 1277960 | tf_op jit(solution)/vmap(transpose(jvp()))/dot_general | solution.py:9
  223.4 12.2 %collective-permute-start.23 = (f32[1,208,512]{2,1,0:T(8,128)S(1)}, f32[1,208,512]{2,1,0:T(8,128)S(1)}, u32[]{:S(2)}, u32[]{:S(2)}) collective-permute-start(f32[1,208,512]{2,1,0:T(8,128)S(1)} %get-tuple-element.501), channel_id=36, source_target_pairs={{0,7},{1,0},{2,1},{3,2},{4,3},{5,4},{6,5},{7,6},{8,15},{9,8},{10,9... | collective-permute-start | bytes 1277960 | tf_op jit(solution)/vmap(transpose(jvp()))/dot_general | solution.py:9
  237.6 11.5 %collective-permute-start.20 = (f32[1,208,512]{2,1,0:T(8,128)S(1)}, f32[1,208,512]{2,1,0:T(8,128)S(1)}, u32[]{:S(2)}, u32[]{:S(2)}) collective-permute-start(f32[1,208,512]{2,1,0:T(8,128)S(1)} %broadcast_select_fusion.34), channel_id=35, source_target_pairs={{0,1},{1,2},{2,3},{3,4},{4,5},{5,6},{6,7},{7,0},{8,9},{9,10},{10,1... | collective-permute-start | bytes 1277960 | tf_op jit(solution)/vmap(transpose(jvp()))/dot_general | solution.py:9
  249.2 10.8 %collective-permute-start.22 = (f32[1,208,512]{2,1,0:T(8,128)S(1)}, f32[1,208,512]{2,1,0:T(8,128)S(1)}, u32[]{:S(2)}, u32[]{:S(2)}) collective-permute-start(f32[1,208,512]{2,1,0:T(8,128)S(1)} %get-tuple-element.500), channel_id=37, source_target_pairs={{0,1},{1,2},{2,3},{3,4},{4,5},{5,6},{6,7},{7,0},{8,9},{9,10},{10,1... | collective-permute-start | bytes 1277960 | tf_op jit(solution)/vmap(transpose(jvp()))/dot_general | solution.py:9
  260.9 370.7 %collective-permute-start.29 = (f32[1,208,512]{2,1,0:T(8,128)}, f32[1,208,512]{2,1,0:T(8,128)}, u32[]{:S(2)}, u32[]{:S(2)}) collective-permute-start(f32[1,208,512]{2,1,0:T(8,128)} %get-tuple-element.47), channel_id=38, source_target_pairs={{0,1},{1,2},{2,3},{3,4},{4,5},{5,6},{6,7},{7,0},{8,9},{9,10},{10,1... | collective-permute-start | bytes 1277960 | tf_op jit(solution)/vmap(transpose(jvp()))/dot_general | solution.py:9
  311.5 11.3 %collective-permute-start.16 = (f32[1,208,512]{2,1,0:T(8,128)S(1)}, f32[1,208,512]{2,1,0:T(8,128)S(1)}, u32[]{:S(2)}, u32[]{:S(2)}) collective-permute-start(f32[1,208,512]{2,1,0:T(8,128)S(1)} %broadcast_select_fusion.32), channel_id=29, source_target_pairs={{0,1},{1,2},{2,3},{3,4},{4,5},{5,6},{6,7},{7,0},{8,9},{9,10},{10,1... | collective-permute-start | bytes 1277960 | tf_op jit(solution)/vmap(transpose(jvp()))/dot_general | solution.py:9
  334.3 11.3 %collective-permute-start.16 = (f32[1,208,512]{2,1,0:T(8,128)S(1)}, f32[1,208,512]{2,1,0:T(8,128)S(1)}, u32[]{:S(2)}, u32[]{:S(2)}) collective-permute-start(f32[1,208,512]{2,1,0:T(8,128)S(1)} %broadcast_select_fusion.32), channel_id=29, source_target_pairs={{0,1},{1,2},{2,3},{3,4},{4,5},{5,6},{6,7},{7,0},{8,9},{9,10},{10,1... | collective-permute-start | bytes 1277960 | tf_op jit(solution)/vmap(transpose(jvp()))/dot_general | solution.py:9
  345.9 11.2 %collective-permute-start.18 = (f32[1,208,512]{2,1,0:T(8,128)S(1)}, f32[1,208,512]{2,1,0:T(8,128)S(1)}, u32[]{:S(2)}, u32[]{:S(2)}) collective-permute-start(f32[1,208,512]{2,1,0:T(8,128)S(1)} %get-tuple-element.491), channel_id=31, source_target_pairs={{0,1},{1,2},{2,3},{3,4},{4,5},{5,6},{6,7},{7,0},{8,9},{9,10},{10,1... | collective-permute-start | bytes 1277960 | tf_op jit(solution)/vmap(transpose(jvp()))/dot_general | solution.py:9
  358.0 275.2 %collective-permute-start.28 = (f32[1,208,512]{2,1,0:T(8,128)}, f32[1,208,512]{2,1,0:T(8,128)}, u32[]{:S(2)}, u32[]{:S(2)}) collective-permute-start(f32[1,208,512]{2,1,0:T(8,128)} %get-tuple-element.45), channel_id=32, source_target_pairs={{0,1},{1,2},{2,3},{3,4},{4,5},{5,6},{6,7},{7,0},{8,9},{9,10},{10,1... | collective-permute-start | bytes 1277960 | tf_op jit(solution)/vmap(transpose(jvp()))/dot_general | solution.py:9
  397.1 13.3 %collective-permute-start.12 = (f32[1,64,1664]{2,1,0:T(8,128)S(1)}, f32[1,64,1664]{2,1,0:T(8,128)S(1)}, u32[]{:S(2)}, u32[]{:S(2)}) collective-permute-start(f32[1,64,1664]{2,1,0:T(8,128)S(1)} %broadcast_select_fusion.30), channel_id=22, source_target_pairs={{0,1},{1,2},{2,3},{3,4},{4,5},{5,6},{6,7},{7,0},{8,9},{9,10},{10,1... | collective-permute-start | bytes 1277960 | tf_op jit(solution)/vmap(transpose(jvp()))/dot_general | solution.py:21
  399.6 11.2 %collective-permute-start.13 = (f32[1,64,1664]{2,1,0:T(8,128)S(1)}, f32[1,64,1664]{2,1,0:T(8,128)S(1)}, u32[]{:S(2)}, u32[]{:S(2)}) collective-permute-start(f32[1,64,1664]{2,1,0:T(8,128)S(1)} %broadcast_select_fusion.31), channel_id=21, source_target_pairs={{0,7},{1,0},{2,1},{3,2},{4,3},{5,4},{6,5},{7,6},{8,15},{9,8},{10,9... | collective-permute-start | bytes 1277960 | tf_op jit(solution)/vmap(transpose(jvp()))/dot_general | solution.py:21
  410.9 11.7 %collective-permute-start.14 = (f32[1,64,1664]{2,1,0:T(8,128)S(1)}, f32[1,64,1664]{2,1,0:T(8,128)S(1)}, u32[]{:S(2)}, u32[]{:S(2)}) collective-permute-start(f32[1,64,1664]{2,1,0:T(8,128)S(1)} %get-tuple-element.482), channel_id=24, source_target_pairs={{0,1},{1,2},{2,3},{3,4},{4,5},{5,6},{6,7},{7,0},{8,9},{9,10},{10,1... | collective-permute-start | bytes 1277960 | tf_op jit(solution)/vmap(transpose(jvp()))/dot_general | solution.py:21
  411.8 11.1 %collective-permute-start.15 = (f32[1,64,1664]{2,1,0:T(8,128)S(1)}, f32[1,64,1664]{2,1,0:T(8,128)S(1)}, u32[]{:S(2)}, u32[]{:S(2)}) collective-permute-start(f32[1,64,1664]{2,1,0:T(8,128)S(1)} %get-tuple-element.483), channel_id=23, source_target_pairs={{0,7},{1,0},{2,1},{3,2},{4,3},{5,4},{6,5},{7,6},{8,15},{9,8},{10,9... | collective-permute-start | bytes 1277960 | tf_op jit(solution)/vmap(transpose(jvp()))/dot_general | solution.py:21
  424.8 13.3 %collective-permute-start.12 = (f32[1,64,1664]{2,1,0:T(8,128)S(1)}, f32[1,64,1664]{2,1,0:T(8,128)S(1)}, u32[]{:S(2)}, u32[]{:S(2)}) collective-permute-start(f32[1,64,1664]{2,1,0:T(8,128)S(1)} %broadcast_select_fusion.30), channel_id=22, source_target_pairs={{0,1},{1,2},{2,3},{3,4},{4,5},{5,6},{6,7},{7,0},{8,9},{9,10},{10,1... | collective-permute-start | bytes 1277960 | tf_op jit(solution)/vmap(transpose(jvp()))/dot_general | solution.py:21
  424.9 13.2 %collective-permute-start.13 = (f32[1,64,1664]{2,1,0:T(8,128)S(1)}, f32[1,64,1664]{2,1,0:T(8,128)S(1)}, u32[]{:S(2)}, u32[]{:S(2)}) collective-permute-start(f32[1,64,1664]{2,1,0:T(8,128)S(1)} %broadcast_select_fusion.31), channel_id=21, source_target_pairs={{0,7},{1,0},{2,1},{3,2},{4,3},{5,4},{6,5},{7,6},{8,15},{9,8},{10,9... | collective-permute-start | bytes 1277960 | tf_op jit(solution)/vmap(transpose(jvp()))/dot_general | solution.py:21
  438.2 13.2 %collective-permute-start.14 = (f32[1,64,1664]{2,1,0:T(8,128)S(1)}, f32[1,64,1664]{2,1,0:T(8,128)S(1)}, u32[]{:S(2)}, u32[]{:S(2)}) collective-permute-start(f32[1,64,1664]{2,1,0:T(8,128)S(1)} %get-tuple-element.482), channel_id=24, source_target_pairs={{0,1},{1,2},{2,3},{3,4},{4,5},{5,6},{6,7},{7,0},{8,9},{9,10},{10,1... | collective-permute-start | bytes 1277960 | tf_op jit(solution)/vmap(transpose(jvp()))/dot_general | solution.py:21
  439.1 12.3 %collective-permute-start.15 = (f32[1,64,1664]{2,1,0:T(8,128)S(1)}, f32[1,64,1664]{2,1,0:T(8,128)S(1)}, u32[]{:S(2)}, u32[]{:S(2)}) collective-permute-start(f32[1,64,1664]{2,1,0:T(8,128)S(1)} %get-tuple-element.483), channel_id=23, source_target_pairs={{0,7},{1,0},{2,1},{3,2},{4,3},{5,4},{6,5},{7,6},{8,15},{9,8},{10,9... | collective-permute-start | bytes 1277960 | tf_op jit(solution)/vmap(transpose(jvp()))/dot_general | solution.py:21
  452.3 182.8 %collective-permute-start.27 = (f32[1,64,1664]{2,1,0:T(8,128)}, f32[1,64,1664]{2,1,0:T(8,128)}, u32[]{:S(2)}, u32[]{:S(2)}) collective-permute-start(f32[1,64,1664]{2,1,0:T(8,128)} %get-tuple-element.43), channel_id=25, source_target_pairs={{0,1},{1,2},{2,3},{3,4},{4,5},{5,6},{6,7},{7,0},{8,9},{9,10},{10,1... | collective-permute-start | bytes 1277960 | tf_op jit(solution)/vmap(transpose(jvp()))/dot_general | solution.py:21
  453.0 17.9 %collective-permute-start.8 = (f32[1,64,1664]{2,1,0:T(8,128)S(1)}, f32[1,64,1664]{2,1,0:T(8,128)S(1)}, u32[]{:S(2)}, u32[]{:S(2)}) collective-permute-start(f32[1,64,1664]{2,1,0:T(8,128)S(1)} %broadcast_select_fusion.28), channel_id=16, source_target_pairs={{0,1},{1,2},{2,3},{3,4},{4,5},{5,6},{6,7},{7,0},{8,9},{9,10},{10,1... | collective-permute-start | bytes 1277960 | tf_op jit(solution)/vmap(transpose(jvp()))/dot_general | solution.py:21
  455.9 15.0 %collective-permute-start.9 = (f32[1,64,1664]{2,1,0:T(8,128)}, f32[1,64,1664]{2,1,0:T(8,128)S(1)}, u32[]{:S(2)}, u32[]{:S(2)}) collective-permute-start(f32[1,64,1664]{2,1,0:T(8,128)} %broadcast_select_fusion.29), channel_id=15, source_target_pairs={{0,7},{1,0},{2,1},{3,2},{4,3},{5,4},{6,5},{7,6},{8,15},{9,8},{10,9... | collective-permute-start | bytes 1277960 | tf_op jit(solution)/vmap(transpose(jvp()))/dot_general | solution.py:21
  471.0 13.7 %collective-permute-start.10 = (f32[1,64,1664]{2,1,0:T(8,128)S(1)}, f32[1,64,1664]{2,1,0:T(8,128)S(1)}, u32[]{:S(2)}, u32[]{:S(2)}) collective-permute-start(f32[1,64,1664]{2,1,0:T(8,128)S(1)} %get-tuple-element.473), channel_id=18, source_target_pairs={{0,1},{1,2},{2,3},{3,4},{4,5},{5,6},{6,7},{7,0},{8,9},{9,10},{10,1... | collective-permute-start | bytes 1277960 | tf_op jit(solution)/vmap(transpose(jvp()))/dot_general | solution.py:21
  471.1 13.6 %collective-permute-start.11 = (f32[1,64,1664]{2,1,0:T(8,128)S(1)}, f32[1,64,1664]{2,1,0:T(8,128)S(1)}, u32[]{:S(2)}, u32[]{:S(2)}) collective-permute-start(f32[1,64,1664]{2,1,0:T(8,128)S(1)} %get-tuple-element.474), channel_id=17, source_target_pairs={{0,7},{1,0},{2,1},{3,2},{4,3},{5,4},{6,5},{7,6},{8,15},{9,8},{10,9... | collective-permute-start | bytes 1277960 | tf_op jit(solution)/vmap(transpose(jvp()))/dot_general | solution.py:21
  486.6 14.0 %collective-permute-start.8 = (f32[1,64,1664]{2,1,0:T(8,128)S(1)}, f32[1,64,1664]{2,1,0:T(8,128)S(1)}, u32[]{:S(2)}, u32[]{:S(2)}) collective-permute-start(f32[1,64,1664]{2,1,0:T(8,128)S(1)} %broadcast_select_fusion.28), channel_id=16, source_target_pairs={{0,1},{1,2},{2,3},{3,4},{4,5},{5,6},{6,7},{7,0},{8,9},{9,10},{10,1... | collective-permute-start | bytes 1277960 | tf_op jit(solution)/vmap(transpose(jvp()))/dot_general | solution.py:21
  487.7 12.9 %collective-permute-start.9 = (f32[1,64,1664]{2,1,0:T(8,128)}, f32[1,64,1664]{2,1,0:T(8,128)S(1)}, u32[]{:S(2)}, u32[]{:S(2)}) collective-permute-start(f32[1,64,1664]{2,1,0:T(8,128)} %broadcast_select_fusion.29), channel_id=15, source_target_pairs={{0,7},{1,0},{2,1},{3,2},{4,3},{5,4},{6,5},{7,6},{8,15},{9,8},{10,9... | collective-permute-start | bytes 1277960 | tf_op jit(solution)/vmap(transpose(jvp()))/dot_general | solution.py:21
  500.8 10.6 %collective-permute-start.10 = (f32[1,64,1664]{2,1,0:T(8,128)S(1)}, f32[1,64,1664]{2,1,0:T(8,128)S(1)}, u32[]{:S(2)}, u32[]{:S(2)}) collective-permute-start(f32[1,64,1664]{2,1,0:T(8,128)S(1)} %get-tuple-element.473), channel_id=18, source_target_pairs={{0,1},{1,2},{2,3},{3,4},{4,5},{5,6},{6,7},{7,0},{8,9},{9,10},{10,1... | collective-permute-start | bytes 1277960 | tf_op jit(solution)/vmap(transpose(jvp()))/dot_general | solution.py:21
  500.9 10.5 %collective-permute-start.11 = (f32[1,64,1664]{2,1,0:T(8,128)S(1)}, f32[1,64,1664]{2,1,0:T(8,128)S(1)}, u32[]{:S(2)}, u32[]{:S(2)}) collective-permute-start(f32[1,64,1664]{2,1,0:T(8,128)S(1)} %get-tuple-element.474), channel_id=17, source_target_pairs={{0,7},{1,0},{2,1},{3,2},{4,3},{5,4},{6,5},{7,6},{8,15},{9,8},{10,9... | collective-permute-start | bytes 1277960 | tf_op jit(solution)/vmap(transpose(jvp()))/dot_general | solution.py:21
  512.3 13.3 %collective-permute-start.4 = (f32[1,64,1664]{2,1,0:T(8,128)S(1)}, f32[1,64,1664]{2,1,0:T(8,128)S(1)}, u32[]{:S(2)}, u32[]{:S(2)}) collective-permute-start(f32[1,64,1664]{2,1,0:T(8,128)S(1)} %broadcast_select_fusion.26), channel_id=9, source_target_pairs={{0,1},{1,2},{2,3},{3,4},{4,5},{5,6},{6,7},{7,0},{8,9},{9,10},{10,1... | collective-permute-start | bytes 1277960 | tf_op jit(solution)/vmap(transpose(jvp()))/dot_general | solution.py:20
  512.5 13.2 %collective-permute-start.5 = (f32[1,64,1664]{2,1,0:T(8,128)S(1)}, f32[1,64,1664]{2,1,0:T(8,128)S(1)}, u32[]{:S(2)}, u32[]{:S(2)}) collective-permute-start(f32[1,64,1664]{2,1,0:T(8,128)S(1)} %broadcast_select_fusion.27), channel_id=8, source_target_pairs={{0,7},{1,0},{2,1},{3,2},{4,3},{5,4},{6,5},{7,6},{8,15},{9,8},{10,9... | collective-permute-start | bytes 1277960 | tf_op jit(solution)/vmap(transpose(jvp()))/dot_general | solution.py:20
  525.7 10.6 %collective-permute-start.6 = (f32[1,64,1664]{2,1,0:T(8,128)S(1)}, f32[1,64,1664]{2,1,0:T(8,128)S(1)}, u32[]{:S(2)}, u32[]{:S(2)}) collective-permute-start(f32[1,64,1664]{2,1,0:T(8,128)S(1)} %get-tuple-element.464), channel_id=11, source_target_pairs={{0,1},{1,2},{2,3},{3,4},{4,5},{5,6},{6,7},{7,0},{8,9},{9,10},{10,1... | collective-permute-start | bytes 1277960 | tf_op jit(solution)/vmap(transpose(jvp()))/dot_general | solution.py:20
  525.8 10.5 %collective-permute-start.7 = (f32[1,64,1664]{2,1,0:T(8,128)S(1)}, f32[1,64,1664]{2,1,0:T(8,128)}, u32[]{:S(2)}, u32[]{:S(2)}) collective-permute-start(f32[1,64,1664]{2,1,0:T(8,128)S(1)} %get-tuple-element.465), channel_id=10, source_target_pairs={{0,7},{1,0},{2,1},{3,2},{4,3},{5,4},{6,5},{7,6},{8,15},{9,8},{10,9... | collective-permute-start | bytes 1277960 | tf_op jit(solution)/vmap(transpose(jvp()))/dot_general | solution.py:20
  539.3 13.3 %collective-permute-start.4 = (f32[1,64,1664]{2,1,0:T(8,128)S(1)}, f32[1,64,1664]{2,1,0:T(8,128)S(1)}, u32[]{:S(2)}, u32[]{:S(2)}) collective-permute-start(f32[1,64,1664]{2,1,0:T(8,128)S(1)} %broadcast_select_fusion.26), channel_id=9, source_target_pairs={{0,1},{1,2},{2,3},{3,4},{4,5},{5,6},{6,7},{7,0},{8,9},{9,10},{10,1... | collective-permute-start | bytes 1277960 | tf_op jit(solution)/vmap(transpose(jvp()))/dot_general | solution.py:20
  539.4 13.2 %collective-permute-start.5 = (f32[1,64,1664]{2,1,0:T(8,128)S(1)}, f32[1,64,1664]{2,1,0:T(8,128)S(1)}, u32[]{:S(2)}, u32[]{:S(2)}) collective-permute-start(f32[1,64,1664]{2,1,0:T(8,128)S(1)} %broadcast_select_fusion.27), channel_id=8, source_target_pairs={{0,7},{1,0},{2,1},{3,2},{4,3},{5,4},{6,5},{7,6},{8,15},{9,8},{10,9... | collective-permute-start | bytes 1277960 | tf_op jit(solution)/vmap(transpose(jvp()))/dot_general | solution.py:20
  552.7 10.6 %collective-permute-start.6 = (f32[1,64,1664]{2,1,0:T(8,128)S(1)}, f32[1,64,1664]{2,1,0:T(8,128)S(1)}, u32[]{:S(2)}, u32[]{:S(2)}) collective-permute-start(f32[1,64,1664]{2,1,0:T(8,128)S(1)} %get-tuple-element.464), channel_id=11, source_target_pairs={{0,1},{1,2},{2,3},{3,4},{4,5},{5,6},{6,7},{7,0},{8,9},{9,10},{10,1... | collective-permute-start | bytes 1277960 | tf_op jit(solution)/vmap(transpose(jvp()))/dot_general | solution.py:20
  566.3 14.1 %collective-permute-start = (f32[1,64,1664]{2,1,0:T(8,128)}, f32[1,64,1664]{2,1,0:T(8,128)}, u32[]{:S(2)}, u32[]{:S(2)}) collective-permute-start(f32[1,64,1664]{2,1,0:T(8,128)} %broadcast_select_fusion.24), channel_id=3, source_target_pairs={{0,1},{1,2},{2,3},{3,4},{4,5},{5,6},{6,7},{7,0},{8,9},{9,10},{10,1... | collective-permute-start | bytes 1277960 | tf_op jit(solution)/vmap(transpose(jvp()))/dot_general | solution.py:20
  567.1 13.3 %collective-permute-start.1 = (f32[1,64,1664]{2,1,0:T(8,128)}, f32[1,64,1664]{2,1,0:T(8,128)S(1)}, u32[]{:S(2)}, u32[]{:S(2)}) collective-permute-start(f32[1,64,1664]{2,1,0:T(8,128)} %broadcast_select_fusion.25), channel_id=2, source_target_pairs={{0,7},{1,0},{2,1},{3,2},{4,3},{5,4},{6,5},{7,6},{8,15},{9,8},{10,9... | collective-permute-start | bytes 1277960 | tf_op jit(solution)/vmap(transpose(jvp()))/dot_general | solution.py:20
  582.4 10.5 %collective-permute-start.2 = (f32[1,64,1664]{2,1,0:T(8,128)}, f32[1,64,1664]{2,1,0:T(8,128)S(1)}, u32[]{:S(2)}, u32[]{:S(2)}) collective-permute-start(f32[1,64,1664]{2,1,0:T(8,128)} %get-tuple-element.455), channel_id=5, source_target_pairs={{0,1},{1,2},{2,3},{3,4},{4,5},{5,6},{6,7},{7,0},{8,9},{9,10},{10,1... | collective-permute-start | bytes 1277960 | tf_op jit(solution)/vmap(transpose(jvp()))/dot_general | solution.py:20
  582.4 11.3 %collective-permute-start.3 = (f32[1,64,1664]{2,1,0:T(8,128)}, f32[1,64,1664]{2,1,0:T(8,128)}, u32[]{:S(2)}, u32[]{:S(2)}) collective-permute-start(f32[1,64,1664]{2,1,0:T(8,128)} %get-tuple-element.456), channel_id=4, source_target_pairs={{0,7},{1,0},{2,1},{3,2},{4,3},{5,4},{6,5},{7,6},{8,15},{9,8},{10,9... | collective-permute-start | bytes 1277960 | tf_op jit(solution)/vmap(transpose(jvp()))/dot_general | solution.py:20
  597.4 14.1 %collective-permute-start = (f32[1,64,1664]{2,1,0:T(8,128)}, f32[1,64,1664]{2,1,0:T(8,128)}, u32[]{:S(2)}, u32[]{:S(2)}) collective-permute-start(f32[1,64,1664]{2,1,0:T(8,128)} %broadcast_select_fusion.24), channel_id=3, source_target_pairs={{0,1},{1,2},{2,3},{3,4},{4,5},{5,6},{6,7},{7,0},{8,9},{9,10},{10,1... | collective-permute-start | bytes 1277960 | tf_op jit(solution)/vmap(transpose(jvp()))/dot_general | solution.py:20
  598.2 13.3 %collective-permute-start.1 = (f32[1,64,1664]{2,1,0:T(8,128)}, f32[1,64,1664]{2,1,0:T(8,128)S(1)}, u32[]{:S(2)}, u32[]{:S(2)}) collective-permute-start(f32[1,64,1664]{2,1,0:T(8,128)} %broadcast_select_fusion.25), channel_id=2, source_target_pairs={{0,7},{1,0},{2,1},{3,2},{4,3},{5,4},{6,5},{7,6},{8,15},{9,8},{10,9... | collective-permute-start | bytes 1277960 | tf_op jit(solution)/vmap(transpose(jvp()))/dot_general | solution.py:20
  613.5 13.9 %collective-permute-start.2 = (f32[1,64,1664]{2,1,0:T(8,128)}, f32[1,64,1664]{2,1,0:T(8,128)S(1)}, u32[]{:S(2)}, u32[]{:S(2)}) collective-permute-start(f32[1,64,1664]{2,1,0:T(8,128)} %get-tuple-element.455), channel_id=5, source_target_pairs={{0,1},{1,2},{2,3},{3,4},{4,5},{5,6},{6,7},{7,0},{8,9},{9,10},{10,1... | collective-permute-start | bytes 1277960 | tf_op jit(solution)/vmap(transpose(jvp()))/dot_general | solution.py:20
  613.5 14.7 %collective-permute-start.3 = (f32[1,64,1664]{2,1,0:T(8,128)}, f32[1,64,1664]{2,1,0:T(8,128)}, u32[]{:S(2)}, u32[]{:S(2)}) collective-permute-start(f32[1,64,1664]{2,1,0:T(8,128)} %get-tuple-element.456), channel_id=4, source_target_pairs={{0,7},{1,0},{2,1},{3,2},{4,3},{5,4},{6,5},{7,6},{8,15},{9,8},{10,9... | collective-permute-start | bytes 1277960 | tf_op jit(solution)/vmap(transpose(jvp()))/dot_general | solution.py:20
  631.5 12.7 %collective-permute-start.25 = (f32[1,64,1664]{2,1,0:T(8,128)}, f32[1,64,1664]{2,1,0:T(8,128)S(1)}, u32[]{:S(2)}, u32[]{:S(2)}) collective-permute-start(f32[1,64,1664]{2,1,0:T(8,128)} %get-tuple-element.39), channel_id=12, source_target_pairs={{0,1},{1,2},{2,3},{3,4},{4,5},{5,6},{6,7},{7,0},{8,9},{9,10},{10,1... | collective-permute-start | bytes 1277960 | tf_op jit(solution)/vmap(transpose(jvp()))/dot_general | solution.py:20
  631.7 17.2 %collective-permute-start.24 = (f32[1,64,1664]{2,1,0:T(8,128)}, f32[1,64,1664]{2,1,0:T(8,128)S(1)}, u32[]{:S(2)}, u32[]{:S(2)}) collective-permute-start(f32[1,64,1664]{2,1,0:T(8,128)} %get-tuple-element.37), channel_id=6, source_target_pairs={{0,1},{1,2},{2,3},{3,4},{4,5},{5,6},{6,7},{7,0},{8,9},{9,10},{10,1... | collective-permute-start | bytes 1277960 | tf_op jit(solution)/vmap(transpose(jvp()))/dot_general | solution.py:20
  671.1 87.8 %all-gather.12.cloned.1.call-start = ((), (), s32[]{:S(2)}) async-start(), calls=%async_computation.1 | async-start | bytes 3833856 | tf_op jit(solution)/reshape | solution.py:58
  674.3 129.4 %all-gather.10.cloned.1.call-start = ((), (), s32[]{:S(2)}) async-start(), calls=%async_computation | async-start | bytes 3833856 | tf_op jit(solution)/reshape | solution.py:58
  (40 other events, 688.7 us)
Sparse Core Ops, SparseCore 0:
  671.2 42.8 all-gather.13
  716.3 42.5 all-gather.11
  761.1 42.5 all-gather.9
where the time goes:
time: 829 us; the launch traced here: 818 us
  matrix products  323 us (39%)
  waiting for transfers between devices  177 us (21%)
  starting transfers between devices  87.6 us (11%)
  local copies, waits for them, and re-layouts  86.6 us (10%)
  other arithmetic  86.5 us (10%)
  loops' own time  24.5 us (3%)
  between operations  17.7 us (2%)
  blocking collectives  15.3 us (2%)
    reshape x3, waiting for transfers between devices, step(): t.reshape(-1, *t.shape[2:])  126 us
    dot_general x11, matrix products, layer(): gate = jnp.dot(a, w['w_gate'], preferred_element_type=jnp.float32)  123 us
    dot_general x11, matrix products, layer(): up = jnp.dot(a, w['w_up'], preferred_element_type=jnp.float32)  114 us
    dot_general x11, matrix products, matmul(): jnp.dot(a, w, preferred_element_type=jnp.float32).astype(jnp.bfloat16)  86.4 us
    unnamed x51, local copies, waits for them, and re-layouts  77.1 us
    dot_general x18, starting transfers between devices, matmul(): jnp.dot(a, w, preferred_element_type=jnp.float32).astype(jnp.bfloat16)  32.8 us
    dot_general x18, starting transfers between devices, layer(): up = jnp.dot(a, w['w_up'], preferred_element_type=jnp.float32)  27.6 us
    dot_general x18, starting transfers between devices, layer(): gate = jnp.dot(a, w['w_gate'], preferred_element_type=jnp.float32)  27 us
  transfers between devices with their start and end apart: 57, of which 19 were waited for; matrix products, arithmetic and copies ran while one was open for 34% of the time, Pallas kernels for 0%

commit v1 on v0

v1 whole, which is shorter than its diff:
```python
import functools

import jax
import jax.numpy as jnp
from jax import lax
from jax.experimental import pallas as pl
from jax.experimental.pallas import tpu as pltpu
from jax.sharding import PartitionSpec as P

F32, BF16 = jnp.float32, jnp.bfloat16
MESH = pl.DeviceIdType.MESH
TILE = 256
VMEM_LIMIT = 63 * 1024 * 1024


def dot(a, b, dims):
    return lax.dot_general(a, b, (dims, ((), ())), preferred_element_type=F32)


NN, NT, TN = ((1,), (0,)), ((1,), (1,)), ((0,), (0,))


def scale_of(wide):
    return lax.rsqrt(jnp.mean(wide * wide, -1, keepdims=True) + 1e-6)


def first_kernel(x_ref, dy_ref, wg_ref, wu_ref, wd_ref, gate_ref, up_ref, h_ref, dg_ref, du_ref, og_ref, ou_ref, od_ref, ag_ref, au_ref, ad_ref):
    step, last = pl.program_id(0), pl.num_programs(0) - 1

    @pl.when(step == 0)
    def _():
        for ref in (ag_ref, au_ref, ad_ref):
            ref[...] = jnp.zeros_like(ref)

    x = x_ref[...]
    wide = x.astype(F32)
    a = (wide * scale_of(wide)).astype(BF16)
    gate = dot(a, wg_ref[0], NN)
    up = dot(a, wu_ref[0], NN)
    gate_ref[...] = gate
    up_ref[...] = up
    act = (gate * jax.nn.sigmoid(gate) * up).astype(BF16)
    h = x + dot(act, wd_ref[0], NN).astype(BF16)
    h_ref[...] = h
    wide = h.astype(F32)
    a = (wide * scale_of(wide)).astype(BF16)
    dy = dy_ref[...]
    dact = dot(dy, wd_ref[1], NT).astype(BF16).astype(F32)
    gate = dot(a, wg_ref[1], NN)
    up = dot(a, wu_ref[1], NN)
    s = jax.nn.sigmoid(gate)
    silu = gate * s
    act = (silu * up).astype(BF16)
    dg = (dact * up * (s * (1.0 + gate * (1.0 - s)))).astype(BF16)
    du = (dact * silu).astype(BF16)
    dg_ref[...] = dg
    du_ref[...] = du
    ad_ref[...] += dot(act, dy, TN)
    ag_ref[...] += dot(a, dg, TN)
    au_ref[...] += dot(a, du, TN)

    @pl.when(step == last)
    def _():
        og_ref[...] = ag_ref[...].astype(BF16)
        ou_ref[...] = au_ref[...].astype(BF16)
        od_ref[...] = ad_ref[...].astype(BF16)


def second_kernel(x_ref, dy_ref, wg_ref, wu_ref, wd_ref, gate_ref, up_ref, h_ref, dg_ref, du_ref, og_ref, ou_ref, od_ref, ag_ref, au_ref, ad_ref):
    step, last = pl.program_id(0), pl.num_programs(0) - 1

    @pl.when(step == 0)
    def _():
        for ref in (ag_ref, au_ref, ad_ref):
            ref[...] = jnp.zeros_like(ref)

    da = dot(dg_ref[...], wg_ref[0], NT).astype(BF16) + dot(du_ref[...], wu_ref[0], NT).astype(BF16)
    da = da.astype(F32)
    wide = h_ref[...].astype(F32)
    scale = scale_of(wide)
    inner = jnp.mean(da * wide, -1, keepdims=True)
    dh = dy_ref[...] + (scale * da - wide * (scale * scale * scale * inner)).astype(BF16)
    dact = dot(dh, wd_ref[0], NT).astype(BF16).astype(F32)
    gate, up = gate_ref[...], up_ref[...]
    s = jax.nn.sigmoid(gate)
    silu = gate * s
    act = (silu * up).astype(BF16)
    dg = (dact * up * (s * (1.0 + gate * (1.0 - s)))).astype(BF16)
    du = (dact * silu).astype(BF16)
    wide = x_ref[...].astype(F32)
    a = (wide * scale_of(wide)).astype(BF16)
    ad_ref[...] += dot(act, dh, TN)
    ag_ref[...] += dot(a, dg, TN)
    au_ref[...] += dot(a, du, TN)

    @pl.when(step == last)
    def _():
        og_ref[...] = ag_ref[...].astype(BF16)
        ou_ref[...] = au_ref[...].astype(BF16)
        od_ref[...] = ad_ref[...].astype(BF16)


def chains_of(layers, shapes, n):
    chains = []
    for layer in layers:
        for k, (rows, _) in enumerate(shapes):
            block = rows // n
            cut = -(-(block // 2) // 16) * 16
            if layer % 2:
                cut = block - cut
            chains.append((layer, k, 0, block, 0, cut))
            chains.append((layer, k, 1, block, cut, block - cut))
    return chains


def tail_kernel(
    n, count, chains,
    t00, t01, t02, t10, t11, t12, w0, w1, w2, m0, m1, m2, v0, v1, v2,
    o0, o1, o2, om0, om1, om2, ov0, ov1, ov2,
    wide_recv, tall_recv, g0, g1, g2, wb0, wb1, wb2, part, parts, send_sem, recv_sem, gsend_sem, grecv_sem, psend_sem, precv_sem, local_sem,
):
    me = lax.axis_index("dp")
    terms, w, m, v = ((t00, t01, t02), (t10, t11, t12)), (w0, w1, w2), (m0, m1, m2), (v0, v1, v2)
    out, om, ov, g, wb = (o0, o1, o2), (om0, om1, om2), (ov0, ov1, ov2), (g0, g1, g2), (wb0, wb1, wb2)
    fetches = []
    for k in range(3):
        block = wb[k].shape[1]
        fetches.append(pltpu.make_async_copy(w[k].at[:, pl.ds(pl.multiple_of(me * block, 16), block), :], wb[k], local_sem.at[k]))
    for f in fetches:
        f.start()

    barrier = pltpu.get_barrier_semaphore()
    for d in range(1, n):
        pl.semaphore_signal(barrier, inc=1, device_id={"dp": lax.rem(me + d, n)}, device_id_type=MESH)
    pl.semaphore_wait(barrier, n - 1)

    def peer(way):
        return {"dp": lax.rem(me + (1 if way == 0 else n - 1), n)}

    def rows(chain, owner):
        _, _, _, block, off, size = chain
        return pl.ds(pl.multiple_of(owner * block + off, 16), size)

    def owner(way, s):
        return lax.rem(me + (2 * n - 1 - s if way == 0 else 1 + s), n)

    def slot(i, s):
        _, k, _, _, _, size = chains[i]
        return (wide_recv if k < 2 else tall_recv).at[index[i], s, pl.ds(0, size)]

    index, seen = [], [0, 0]
    for c in chains:
        kind = 0 if c[1] < 2 else 1
        index.append(seen[kind])
        seen[kind] += 1

    def copy(i, src, s):
        return pltpu.make_async_remote_copy(
            src_ref=src, dst_ref=slot(i, s), send_sem=send_sem.at[i, s], recv_sem=recv_sem.at[i, s],
            device_id=peer(chains[i][2]), device_id_type=MESH,
        )

    def term(i, which):
        c = chains[i]
        return terms[c[0]][c[1]].at[rows(c, which), :]

    for i, c in enumerate(chains):
        copy(i, term(i, owner(c[2], 0)), 0).start()

    def hop(s, _):
        for i, c in enumerate(chains):
            copy(i, slot(i, s), s).wait_recv()
            total = slot(i, s)[...].astype(F32) + term(i, owner(c[2], s + 1))[...].astype(F32)
            slot(i, s)[...] = total.astype(BF16)
            copy(i, slot(i, s), s + 1).start()
        return 0

    lax.fori_loop(0, n - 2, hop, 0)
    squares = jnp.zeros((), F32)
    for i, c in enumerate(chains):
        layer, k, way, block, off, size = c
        copy(i, slot(i, n - 2), n - 2).wait_recv()
        total = slot(i, n - 2)[...].astype(F32) + term(i, me)[...].astype(F32)
        total = total.astype(BF16)
        g[k][layer, pl.ds(off, size), :] = total
        total = total.astype(F32)
        squares += jnp.sum(total * total)

    part[...] = jnp.full(part.shape, squares, F32)

    def share(d):
        return pltpu.make_async_remote_copy(
            src_ref=part, dst_ref=parts.at[me], send_sem=psend_sem.at[d - 1], recv_sem=precv_sem.at[d - 1],
            device_id={"dp": lax.rem(me + d, n)}, device_id_type=MESH,
        )

    for d in range(1, n):
        share(d).start()
    parts[me] = part[...]
    for f in fetches:
        f.wait()
    for d in range(1, n):
        share(d).wait()
    total = parts[0]
    for d in range(1, n):
        total += parts[d]
    factor = jnp.minimum(1.0, 0.5 * lax.rsqrt(total / count + 1e-30))[0:1, 0:1]

    def spread(i, s, which):
        c = chains[i]
        there = out[c[1]].at[c[0], rows(c, which), :]
        return pltpu.make_async_remote_copy(
            src_ref=there, dst_ref=there, send_sem=gsend_sem.at[i, s], recv_sem=grecv_sem.at[i, s],
            device_id=peer(c[2]), device_id_type=MESH,
        )

    for i, c in enumerate(chains):
        layer, k, way, block, off, size = c
        here = pl.ds(off, size)
        grad = g[k][layer, here, :].astype(F32) * factor
        mm = 0.9 * m[k][layer, here, :] + 0.1 * grad
        vv = 0.95 * v[k][layer, here, :] + 0.05 * grad * grad
        om[k][layer, here, :] = mm
        ov[k][layer, here, :] = vv
        old = wb[k][layer, here, :].astype(F32)
        new = old - 0.02 * (mm * lax.rsqrt(vv + 1e-8) + 0.1 * old)
        out[k][layer, rows(c, me), :] = new.astype(BF16)
        spread(i, 0, me).start()

    def came(way, s):
        return lax.rem(me + (2 * n - 1 - s if way == 0 else 1 + s), n)

    def pass_on(s, _):
        for i, c in enumerate(chains):
            spread(i, s, came(c[2], s)).wait_recv()
            spread(i, s + 1, came(c[2], s)).start()
        return 0

    lax.fori_loop(0, n - 2, pass_on, 0)
    for i, c in enumerate(chains):
        spread(i, n - 2, came(c[2], n - 2)).wait_recv()

    def drain(s, _):
        for i in range(len(chains)):
            copy(i, slot(i, s), s).wait_send()
            spread(i, s, me).wait_send()
        return 0

    lax.fori_loop(0, n - 1, drain, 0)


def on_a_device(n, x, dy, *arrays):
    w, m, v = (arrays[i : i + 3] for i in (0, 3, 6))
    layers, width, hidden = w[0].shape
    x, dy = x.reshape(x.shape[-2:]), dy.reshape(dy.shape[-2:])
    tokens = x.shape[0]

    def tile(cols):
        return pl.BlockSpec((TILE, cols), lambda i: (i, 0))

    def whole(shape, at=None):
        return pl.BlockSpec(shape, lambda i: at or (0,) * len(shape), pipeline_mode=pl.Buffered(1))

    shapes = [(width, hidden), (width, hidden), (hidden, width)]
    flops = 2 * tokens * width * hidden
    grads = [jax.ShapeDtypeStruct(s, BF16) for s in shapes]
    params = pltpu.CompilerParams(dimension_semantics=("arbitrary",), vmem_limit_bytes=VMEM_LIMIT)
    sums = [pltpu.VMEM(s, F32) for s in shapes]
    gate, up, h, dg, du, *late = pl.pallas_call(
        first_kernel,
        grid=(tokens // TILE,),
        in_specs=[tile(width), tile(width), *(whole(t.shape) for t in w)],
        out_specs=[tile(hidden), tile(hidden), tile(width), tile(hidden), tile(hidden), *(whole(s) for s in shapes)],
        out_shape=[
            jax.ShapeDtypeStruct((tokens, hidden), F32), jax.ShapeDtypeStruct((tokens, hidden), F32),
            jax.ShapeDtypeStruct((tokens, width), BF16),
            jax.ShapeDtypeStruct((tokens, hidden), BF16), jax.ShapeDtypeStruct((tokens, hidden), BF16), *grads,
        ],
        scratch_shapes=sums,
        compiler_params=params,
        cost_estimate=pl.CostEstimate(flops=9 * flops, bytes_accessed=16 * tokens * hidden, transcendentals=0),
        name="first",
    )(x, dy, *w)

    early = pl.pallas_call(
        second_kernel,
        grid=(tokens // TILE,),
        in_specs=[
            tile(width), tile(width), whole((1, width, hidden), (1, 0, 0)), whole((1, width, hidden), (1, 0, 0)),
            whole((1, hidden, width)), tile(hidden), tile(hidden), tile(width), tile(hidden), tile(hidden),
        ],
        out_specs=[*(whole(s) for s in shapes)],
        out_shape=grads,
        scratch_shapes=sums,
        compiler_params=params,
        cost_estimate=pl.CostEstimate(flops=6 * flops, bytes_accessed=16 * tokens * hidden, transcendentals=0),
        name="second",
    )(x, dy, *w, gate, up, h, dg, du)

    chains = chains_of(range(layers), shapes, n)
    flat = [c for c in chains if c[1] < 2]
    tall = [c for c in chains if c[1] == 2]
    vmem, hbm = pl.BlockSpec(memory_space=pltpu.VMEM), pl.BlockSpec(memory_space=pl.ANY)
    blocks = [(layers, s[0] // n, s[1]) for s in shapes]
    dma = pltpu.SemaphoreType.DMA
    return pl.pallas_call(
        functools.partial(tail_kernel, n, float(sum(layers * a * b for a, b in shapes)), chains),
        in_specs=[vmem] * 6 + [hbm] * 3 + [vmem] * 6,
        out_specs=[vmem] * 9,
        out_shape=[jax.ShapeDtypeStruct(t.shape, BF16) for t in w] + [jax.ShapeDtypeStruct(b, F32) for b in blocks * 2],
        scratch_shapes=[
            pltpu.VMEM((len(flat), n - 1, max(c[5] for c in flat), hidden), BF16),
            pltpu.VMEM((len(tall), n - 1, max(c[5] for c in tall), width), BF16),
            *(pltpu.VMEM(b, BF16) for b in blocks * 2),
            pltpu.VMEM((8, 128), F32),
            pltpu.VMEM((n, 8, 128), F32),
            dma((len(chains), n - 1)), dma((len(chains), n - 1)), dma((len(chains), n - 1)), dma((len(chains), n - 1)),
            dma((n - 1,)), dma((n - 1,)), dma((3,)),
        ],
        compiler_params=pltpu.CompilerParams(collective_id=0, has_side_effects=True, vmem_limit_bytes=VMEM_LIMIT),
        name="tail",
    )(*early, *late, *w, *m, *v)


def solution(mesh):
    n = mesh.shape["dp"]
    part = P(None, "dp", None)
    whole, split = P("rep", None, None), P("rep", "dp", None)
    return jax.shard_map(
        functools.partial(on_a_device, n),
        mesh=mesh,
        in_specs=(P(("rep", "dp")), P(("rep", "dp")), P(), P(), P(), *([part] * 6)),
        out_specs=(whole,) * 3 + (split,) * 6,
        check_vma=False,
    )
```

time: 829 us -> 395 us (0.48); the launches traced: 818 us -> 395 us
  Pallas kernels: 0 us -> 380 us
  matrix products: 323 us -> 0 us
  waiting for transfers between devices: 177 us -> 0 us
  starting transfers between devices: 87.6 us -> 0 us
  other arithmetic: 86.5 us -> 0 us
  local copies, waits for them, and re-layouts: 86.6 us -> 14.5 us
  loops' own time: 24.5 us -> 0 us
  between operations: 17.7 us -> 0.68 us
  blocking collectives: 15.3 us -> 0 us
    pallas_call x0 -> x3, Pallas kernels: none -> 380 us  [the longest x1 222 us: on_a_device(): pl.pallas_call(functools.partial(tail_kernel, n, float(sum((layers * a *...]
    dot_general x33 -> x0, matrix products: 323 us -> none  [the longest x11 123 us: layer(): gate = jnp.dot(a, w['w_gate'], preferred_element_type=jnp.float32)]
    reshape x3 -> x0, waiting for transfers between devices: 126 us -> none  [step(): t.reshape(-1, *t.shape[2:])]
    dot_general x54 -> x0, starting transfers between devices: 87.4 us -> none  [the longest x18 32.8 us: matmul(): jnp.dot(a, w, preferred_element_type=jnp.float32).astype(jnp.bfloat16)]
    unnamed x51 -> x25, local copies, waits for them, and re-layouts: 77.1 us -> 14.5 us
    dot_general x54 -> x0, waiting for transfers between devices: 51.3 us -> none  [the longest x18 24.9 us: matmul(): jnp.dot(a, w, preferred_element_type=jnp.float32).astype(jnp.bfloat16)]
    dot_general x48 -> x0, other arithmetic: 31.3 us -> none  [the longest x8 11.9 us: layer(): gate = jnp.dot(a, w['w_gate'], preferred_element_type=jnp.float32)]
    convert_element_type x3 -> x0, other arithmetic: 29.7 us -> none  [the longest x1 23.6 us: layer(): (jax.nn.silu(gate) * up).astype(jnp.bfloat16)]
  transfers between devices with their start and end apart: 57 -> 0, of which waited for: 19 -> 0; matrix products, arithmetic and copies ran while one was open for 34% -> 0% of each run, Pallas kernels for 0% -> 0%
where the time goes in v1:
time: 395 us
  Pallas kernels  380 us (96%)
  local copies, waits for them, and re-layouts  14.5 us (4%)
    pallas_call x1, Pallas kernels, on_a_device(): pl.pallas_call(functools.partial(tail_kernel, n, float(sum((layers * a *...  222 us
    pallas_call x1, Pallas kernels, on_a_device(): pl.pallas_call(first_kernel, grid=(tokens // TILE,), in_specs=[tile(width...  89.7 us
    pallas_call x1, Pallas kernels, on_a_device(): pl.pallas_call(second_kernel, grid=(tokens // TILE,), in_specs=[tile(widt...  68.4 us
    unnamed x25, local copies, waits for them, and re-layouts  14.5 us

profile of v1, /device:TPU:22, one launch (start us, length us, event | category | flops | bytes accessed | tf_op | source)
XLA Modules:
  0.0 394.9 jit_solution(10301226919443425588)
XLA Ops:
  0.6 89.7 %first.1 = (f32[4096,1664]{1,0:T(8,128)}, f32[4096,1664]{1,0:T(8,128)}, bf16[4096,512]{1,0:T(8,128)(2,1)}, bf16[4096,1664]{1,0:T(8,128)(2,1)}, bf16[4096,1664]{1...) custom-call(bf16[4096,512]{1,0:T(8,128)(2,1)} %bitcast.2, ...), custom_call_target="tpu_custom_call" | custom-call | flops 62813896704 | bytes 109051904 | tf_op jit(solution)/shard_map/first/pallas_call | solution.py:269
  90.3 68.4 %second.1 = (bf16[512,1664]{1,0:T(8,128)(2,1)}, bf16[512,1664]{1,0:T(8,128)(2,1)}, bf16[1664,512]{1,0:T(8,128)(2,1)}) custom-call(bf16[4096,512]{1,0:T(8,128)(2,1)} %bitcast.3, bf16[4096,512]{1,0:T(8,128)(2,1)} %bitcast.5, bf16[2,512,1664]{2,1,0:T(8,128)(2,1)} %w0.1, bf16[2,512,1664]{2,1,0:T(8,128)(2,1)} %w1.1, bf16[2,1664,512]{2,1,0:T(8,128)(2,1)} %w2.1, ...), custom_call_target="tpu_custom_call" | custom-call | flops 41875931136 | bytes 109051904 | tf_op jit(solution)/shard_map/second/pallas_call | solution.py:285
  158.8 221.7 %tail.1 = (bf16[2,512,1664]{2,1,0:T(8,128)(2,1)}, bf16[2,512,1664]{2,1,0:T(8,128)(2,1)}, bf16[2,1664,512]{2,1,0:T(8,128)(2,1)}, f32[2,64,1664]{2,1,0:T(8,128)}, ...) custom-call(bf16[512,1664]{1,0:T(8,128)(2,1)} %get-tuple-element.25., ...), custom_call_target="tpu_custom_call" | custom-call | tf_op jit(solution)/shard_map/tail/pallas_call | solution.py:306
  380.4 0.0 copy-start.1
  380.4 4.1 %copy.29 = bf16[2,512,1664]{2,1,0:T(8,128)(2,1)} copy(bf16[2,512,1664]{2,1,0:T(8,128)(2,1)} %get-tuple-element.40) | data formatting | bytes 6815744
  384.6 0.0 copy-done.1
  384.6 0.0 copy-start
  384.6 1.8 copy.30
  386.3 1.4 copy-done
  387.7 0.0 copy-start.7
  387.8 0.0 copy-start.6
  387.8 0.0 copy-start.5
  387.8 1.7 copy.31
  389.5 0.0 copy-done.7
  389.5 0.0 copy-start.4
  389.5 0.0 copy-start.3
  389.5 0.9 copy.32
  390.4 0.0 copy-done.6
  390.4 0.0 copy-start.2
  390.4 0.9 copy.33
  391.3 0.0 copy-done.5
  391.3 0.9 copy.34
  392.2 0.0 copy-done.4
  392.2 0.9 copy.35
  393.1 0.0 copy-done.3
  393.1 0.9 copy.36
  394.0 0.0 copy-done.2
  394.0 0.9 copy.37
Async XLA Ops:
  380.4 4.1 %copy-start.1 = (bf16[2,512,1664]{2,1,0:T(8,128)(2,1)S(1)}, bf16[2,512,1664]{2,1,0:T(8,128)(2,1)}, u32[]{:S(2)}) copy-start(bf16[2,512,1664]{2,1,0:T(8,128)(2,1)} %get-tuple-element.41) | copy-start | bytes 10223620
  384.6 3.2 copy-start
  387.7 1.8 copy-start.7
  387.8 2.7 copy-start.6
  387.8 3.6 copy-start.5
  389.5 2.7 copy-start.4
  389.5 3.6 copy-start.3
  390.4 3.6 copy-start.2
